TPU v7x, 32 devices: a whole 2x2x4 slice. The times are simulated.
32 devices in a mesh: row: 4 (over y, core), col: 8 (over z, x).
Axes of the slice: x: 2, y: 2, z: 4, core: 2. Of those that a mesh axis runs over, the one named last changes fastest.
Arguments:
- lower_inverse: float32 [4, 8, 1024, 1024], P('row', 'col'), may hold values from -1 to 2, as said below
- upper_inverse: float32 [4, 8, 1024, 1024], P('row', 'col'), may hold values from -1 to 2, as said below
- left_coupling: bfloat16 [4, 8, 512, 1024], P('row', 'col'), may hold values from -0.1875 to 0.1875
- right_pieces: float32 [8, 1024, 2048], P('col', None, 'row'), may hold values from -6 to 6
- interface_block: int32 [4, 8, 4], P('row', 'col'), may hold values from 0 to 7, all different within a row
- a_gg: float32 [4, 1024, 2048], P('row', 'col'), may hold values from -6 to 6
- panel_order: int32 [4], replicated, may hold values from 0 to 3, each once
Outputs:
- schur: float32 [4, 1024, 2048], P('row', 'col')
Inputs may be any that keep to these rules, and one draw needn't show every extreme that they name: `interface_block`: the 4 block ids of one subdomain are distinct. `panel_order`: A permutation of the column blocks. `lower_inverse`: lower triangular, diagonal between 1 and 2. `upper_inverse`: upper triangular, diagonal between 1 and 2.
All inputs are finite; a program needn't handle non-finite values.
Results may differ from a plain program's by a relative error of at most 0.0028.
Values sent between devices are 32-bit elements; how exact they have to be, the bound alone decides.
A program may use at most 128 MiB of HBM per device.

v0:
```python
import jax
import jax.numpy as jnp
from jax import lax
from jax.sharding import PartitionSpec as P


def column_order(panel_order):
    length = panel_order.shape[0]
    positions = jnp.arange(length, dtype=jnp.int32)
    hits = (panel_order[:, None] == positions[None, :]).astype(jnp.int32)
    return jnp.sum(hits * positions[:, None], axis=0)


def couple(lower_mat, upper_mat, left_mat, panel):
    halfway = jnp.dot(
        lower_mat, panel, precision=lax.Precision.HIGHEST, preferred_element_type=jnp.float32
    )
    solved = jnp.dot(
        upper_mat, halfway, precision=lax.Precision.HIGHEST, preferred_element_type=jnp.float32
    )
    solved = solved.astype(jnp.bfloat16)
    return jnp.dot(left_mat, solved, preferred_element_type=jnp.float32)


def place_rows(coupled, block_ids, block_total):
    block_count = block_ids.shape[0]
    block_rows = coupled.shape[0] // block_count
    targets = jnp.arange(block_total, dtype=jnp.int32)
    placed = (block_ids[:, None] == targets[None, :]).astype(jnp.float32)
    shaped = coupled.reshape(block_count, block_rows, coupled.shape[1])
    spread = jnp.einsum("kb,kwp->bwp", placed, shaped, precision=lax.Precision.HIGHEST)
    return spread.reshape(block_total * block_rows, coupled.shape[1])


def per_device(
    lower_inverse, upper_inverse, left_coupling, right_pieces, interface_block, a_gg, panel_order
):
    lower_mat = lower_inverse[0, 0]
    upper_mat = upper_inverse[0, 0]
    left_mat = left_coupling[0, 0]
    block_ids = interface_block[0, 0]
    row_count = lax.axis_size("row")
    coupled = couple(
        lower_mat, upper_mat, left_mat, lax.all_gather(right_pieces, "row", axis=2, tiled=True)[0]
    )
    order = column_order(panel_order)
    width_piece = right_pieces.shape[2]
    height = coupled.shape[0]
    coupled = coupled.reshape(height, row_count, width_piece)[:, order, :].reshape(
        height, row_count * width_piece
    )
    block_rows = a_gg.shape[1]
    owned = lax.psum_scatter(
        place_rows(coupled, block_ids, block_rows * lax.axis_size("col") // block_rows),
        "col",
        scatter_dimension=0,
        tiled=True,
    )
    return (a_gg[0] - owned)[None]


def solution(mesh):
    return jax.shard_map(
        per_device,
        mesh=mesh,
        in_specs=(
            P("row", "col", None, None),
            P("row", "col", None, None),
            P("row", "col", None, None),
            P("col", None, "row"),
            P("row", "col", None),
            P("row", "col", None),
            P(),
        ),
        out_specs=P("row", "col", None),
        check_vma=False,
    )
```

profile of v0, /device:TPU:0, one launch (start us, length us, event | category | flops | bytes accessed | tf_op | source)
XLA Modules:
  0.0 355.0 jit_solution(11095625044394549900)
XLA Ops:
  6.5 0.0 copy-start
  6.5 0.0 all-gather.2.cloned.1.call-start
  6.5 0.7 all-gather.2.cloned.1.call-update
  7.3 0.0 reduce-scatter.2.cloned.1.call-start
  7.3 0.7 select_reduce_fusion
  8.1 61.9 %all-gather.2.cloned.1.call-done = f32[1,1024,2048]{2,1,0:T(8,128)} async-done(((f32[1,1024,512]{2,1,0:T(8,128)}), f32[1,1024,2048]{2,1,0:T(8,128)}) %all-gather.2.cloned.1.call-update) | async-done | bytes 8388624 | tf_op jit(solution)/shard_map/all_gather | solution.py:44
  69.9 0.0 copy-start.4
  69.9 29.7 %fusion = f32[1024,2048]{1,0:T(8,128)S(1)} fusion(f32[1,1024,2048]{2,1,0:T(8,128)} %all-gather.2.cloned.1.call-done, f32[1,1,1024,1024]{3,2,1,0:T(8,128)} %param.7), kind=kOutput, calls=%fused_computation.1 | convolution fusion | flops 25769803776 | bytes 20971520 | tf_op jit(solution)/shard_map/dot_general | solution.py:15
  99.7 0.0 copy-done.4
  99.7 53.0 %fusion.2 = bf16[2048,1024]{1,0:T(8,128)(2,1)S(1)} fusion(f32[1024,2048]{1,0:T(8,128)S(1)} %fusion, f32[1,1,1024,1024]{3,2,1,0:T(8,128)S(1)} %copy-done.4), kind=kOutput, calls=%fused_computation.3 | convolution fusion | flops 25769803776 | bytes 16777216 | tf_op jit(solution)/shard_map/dot_general | solution.py:18
  152.7 0.0 copy-done
  152.7 4.4 %fusion.7 = f32[2048,512]{1,0:T(8,128)} fusion(bf16[2048,1024]{1,0:T(8,128)(2,1)S(1)} %fusion.2, bf16[1,1,512,1024]{3,2,1,0:T(8,128)(2,1)S(1)} %copy-done), kind=kOutput, calls=%fused_computation.8 | convolution fusion | flops 2147483648 | bytes 9437184 | tf_op jit(solution)/shard_map/dot_general | solution.py:22
  157.0 5.2 %copy.14 = f32[512,4,512]{2,0,1:T(8,128)} copy(f32[512,4,512]{0,2,1:T(8,128)} %bitcast.35) | data formatting | bytes 8388608 | tf_op jit(solution)/shard_map/reshape | solution.py:49
  162.3 5.0 %gather_fusion = f32[4,512,512]{2,1,0:T(8,128)} fusion(f32[512,4,512]{2,0,1:T(8,128)} %copy.14, s32[1024]{0:T(1024)S(1)} %pad_clamp_fusion), kind=kCustom, calls=%fused_computation | custom fusion | bytes 8388624 | tf_op jit(solution)/shard_map/gather | solution.py:49
  167.3 6.8 %copy.15 = f32[512,4,512]{2,1,0:T(4,128)} copy(f32[512,4,512]{2,0,1:T(8,128)} %bitcast.34) | data formatting | bytes 8388608 | tf_op jit(solution)/shard_map/gather | solution.py:49
  174.1 0.0 copy-start.3
  174.1 6.1 %reshape_reshape.3 = f32[4,128,2048]{2,1,0:T(8,128)} reshape(f32[512,4,512]{2,1,0:T(4,128)} %copy.15) | data formatting | bytes 8388608 | tf_op jit(solution)/shard_map/reshape;reshape | solution.py:30
  180.2 0.0 copy-done.3
  180.2 9.9 %fusion.5 = f32[8,128,2048]{2,0,1:T(8,128)S(1)} fusion(f32[4,128,2048]{2,1,0:T(8,128)} %reshape_reshape.3, s32[4]{0:T(128)S(1)} %bitcast.36), kind=kOutput, calls=%fused_computation.6 | convolution fusion | flops 100663328 | bytes 12582928 | tf_op jit(solution)/shard_map/kb,kwp->bwp/dot_general | solution.py:31
  190.1 8.1 %copy.17 = f32[8,128,2048]{2,1,0:T(8,128)} copy(f32[8,128,2048]{2,0,1:T(8,128)S(1)} %fusion.5) | data formatting | bytes 16777216 | tf_op jit(solution)/shard_map/kb,kwp->bwp/dot_general | solution.py:31
  198.2 0.0 copy-start.1
  198.2 0.0 copy-start.2
  198.2 0.0 reduce-scatter.2.cloned.1.call-update
  198.2 147.6 %reduce-scatter.2.cloned.1.call-done = f32[128,2048]{1,0:T(8,128)} async-done(((f32[1024,2048]{1,0:T(8,128)}), f32[128,2048]{1,0:T(8,128)}) %reduce-scatter.2.cloned.1.call-update) | async-done | bytes 1048592 | tf_op jit(solution)/shard_map/reduce_scatter | solution.py:53
  345.8 0.0 copy-done.2
  345.8 2.3 fusion.10
  348.1 0.0 copy-done.1
  (2 shorter events, 0.0 us)
Async XLA Ops:
  6.5 146.1 %copy-start = (bf16[1,1,512,1024]{3,2,1,0:T(8,128)(2,1)S(1)}, bf16[1,1,512,1024]{3,2,1,0:T(8,128)(2,1)}, u32[]{:S(2)}) copy-start(bf16[1,1,512,1024]{3,2,1,0:T(8,128)(2,1)} %param.9) | copy-start | bytes 3145732
  6.5 63.4 %all-gather.2.cloned.1.call-start = ((), (), s32[]{:S(2)}) async-start(), calls=%async_computation.1 | async-start | bytes 10485760 | tf_op jit(solution)/shard_map/all_gather | solution.py:44
  7.3 338.5 %reduce-scatter.2.cloned.1.call-start = ((), (), s32[]{:S(2)}) async-start(), calls=%async_computation.2 | async-start | bytes 9437184 | tf_op jit(solution)/shard_map/reduce_scatter | solution.py:53
  69.9 29.8 %copy-start.4 = (f32[1,1,1024,1024]{3,2,1,0:T(8,128)S(1)}, f32[1,1,1024,1024]{3,2,1,0:T(8,128)}, u32[]{:S(2)}) copy-start(f32[1,1,1024,1024]{3,2,1,0:T(8,128)} %param.8) | copy-start | bytes 12582916
  174.1 6.1 %copy-start.3 = (s32[1,1,4]{2,1,0:T(1,128)S(1)}, s32[1,1,4]{2,1,0:T(1,128)}, u32[]{:S(2)}) copy-start(s32[1,1,4]{2,1,0:T(1,128)} %param.11) | copy-start | bytes 52
  198.2 149.9 %copy-start.1 = (bf16[1,1,512,1024]{3,2,1,0:T(8,128)(2,1)S(1)}, bf16[1,1,512,1024]{3,2,1,0:T(8,128)(2,1)}, u32[]{:S(2)}) copy-start(bf16[1,1,512,1024]{3,2,1,0:T(8,128)(2,1)} %param.9) | copy-start | bytes 3145732
  198.2 147.6 %copy-start.2 = (f32[1,128,2048]{2,1,0:T(8,128)S(1)}, f32[1,128,2048]{2,1,0:T(8,128)}, u32[]{:S(2)}) copy-start(f32[1,128,2048]{2,1,0:T(8,128)} %param.12) | copy-start | bytes 3145732
Sparse Core Ops, SparseCore 0:
  8.9 60.9 all-gather.1
  198.3 147.4 reduce-scatter.1
where the time goes:
time: 355 us
  waiting for transfers between devices  210 us (59%)
  matrix products  97 us (27%)
  local copies, waits for them, and re-layouts  31.2 us (9%)
  between operations  13.4 us (4%)
    reduce_scatter x1, waiting for transfers between devices, per_device(): lax.psum_scatter(place_rows(coupled, block_ids, block_rows * lax.axis_siz...  148 us
    all_gather x1, waiting for transfers between devices, per_device(): lax.all_gather(right_pieces, 'row', axis=2, tiled=True)[0]  61.9 us
    dot_general x1, matrix products, couple(): jnp.dot(upper_mat, halfway, precision=lax.Precision.HIGHEST, preferred_el...  53 us
    dot_general x1, matrix products, couple(): jnp.dot(lower_mat, panel, precision=lax.Precision.HIGHEST, preferred_elem...  29.7 us
    gather x2, local copies, waits for them, and re-layouts, per_device(): coupled.reshape(height, row_count, width_piece)[:, order, :]  11.8 us
    dot_general x1, matrix products, place_rows(): jnp.einsum('kb,kwp->bwp', placed, shaped, precision=lax.Precision.HIGHEST)  9.92 us
    dot_general x1, local copies, waits for them, and re-layouts, place_rows(): jnp.einsum('kb,kwp->bwp', placed, shaped, precision=lax.Precision.HIGHEST)  8.08 us
  transfers between devices with their start and end apart: 2, of which 2 were waited for; matrix products, arithmetic and copies ran while one was open for 0% of the time, Pallas kernels for 0%

commit v1 on v0

--- a/solution.py
+++ b/solution.py
@@ -2,6 +2,11 @@
 import jax.numpy as jnp
 from jax import lax
 from jax.sharding import PartitionSpec as P
+
+
+def stack_and_merge(array, axis, dim):
+    tiles = lax.all_gather(array, axis)
+    return jnp.concatenate(tiles, axis=dim)
 
 
 def column_order(panel_order):
@@ -40,9 +45,7 @@
     left_mat = left_coupling[0, 0]
     block_ids = interface_block[0, 0]
     row_count = lax.axis_size("row")
-    coupled = couple(
-        lower_mat, upper_mat, left_mat, lax.all_gather(right_pieces, "row", axis=2, tiled=True)[0]
-    )
+    coupled = couple(lower_mat, upper_mat, left_mat, stack_and_merge(right_pieces, "row", 2)[0])
     order = column_order(panel_order)
     width_piece = right_pieces.shape[2]
     height = coupled.shape[0]

time: 355 us -> 370 us (1.042); the launches traced: 355 us -> 364 us
  local copies, waits for them, and re-layouts: 31.2 us -> 39.9 us
    all_gather x0 -> x1, local copies, waits for them, and re-layouts: none -> 8.73 us  [stack_and_merge(): tiles = lax.all_gather(array, axis)]
where the time goes in v1:
time: 370 us; the launch traced here: 364 us
  waiting for transfers between devices  210 us (57%)
  matrix products  97.3 us (26%)
  local copies, waits for them, and re-layouts  39.9 us (11%)
  between operations  13.7 us (4%)
    reduce_scatter x1, waiting for transfers between devices, per_device(): lax.psum_scatter(place_rows(coupled, block_ids, block_rows * lax.axis_siz...  148 us
    all_gather x1, waiting for transfers between devices, stack_and_merge(): tiles = lax.all_gather(array, axis)  61.9 us
    dot_general x1, matrix products, couple(): jnp.dot(upper_mat, halfway, precision=lax.Precision.HIGHEST, preferred_el...  53.2 us
    dot_general x1, matrix products, couple(): jnp.dot(lower_mat, panel, precision=lax.Precision.HIGHEST, preferred_elem...  29.8 us
    gather x2, local copies, waits for them, and re-layouts, per_device(): coupled.reshape(height, row_count, width_piece)[:, order, :]  11.8 us
    dot_general x1, matrix products, place_rows(): jnp.einsum('kb,kwp->bwp', placed, shaped, precision=lax.Precision.HIGHEST)  9.86 us
    all_gather x1, local copies, waits for them, and re-layouts, stack_and_merge(): tiles = lax.all_gather(array, axis)  8.73 us
    dot_general x1, local copies, waits for them, and re-layouts, place_rows(): jnp.einsum('kb,kwp->bwp', placed, shaped, precision=lax.Precision.HIGHEST)  8.08 us
  transfers between devices with their start and end apart: 2, of which 2 were waited for; matrix products, arithmetic and copies ran while one was open for 0% of the time, Pallas kernels for 0%

profile of v1, /device:TPU:0, one launch (start us, length us, event | category | flops | bytes accessed | tf_op | source)
XLA Modules:
  0.0 364.2 jit_solution(5811372967575138404)
XLA Ops:
  6.5 0.0 copy-start
  6.5 0.0 all-gather.3.cloned.1.call-start
  6.5 0.7 all-gather.3.cloned.1.call-update
  7.3 0.0 reduce-scatter.2.cloned.1.call-start
  7.3 0.7 select_reduce_fusion
  8.1 61.9 %all-gather.3.cloned.1.call-done = f32[4,1024,512]{2,1,0:T(8,128)} async-done(((f32[1,1024,512]{2,1,0:T(8,128)}), f32[4,1024,512]{2,1,0:T(8,128)}) %all-gather.3.cloned.1.call-update) | async-done | bytes 8388624 | tf_op jit(solution)/shard_map/all_gather | solution.py:8
  69.9 8.7 %copy.21 = f32[4,1024,512]{1,2,0:T(8,128)} copy(f32[4,1024,512]{2,1,0:T(8,128)} %all-gather.3.cloned.1.call-done) | data formatting | bytes 16777216 | tf_op jit(solution)/shard_map/all_gather | solution.py:8
  78.6 0.0 copy-start.4
  78.6 29.8 %fusion.2 = f32[1024,2048]{1,0:T(8,128)S(1)} fusion(f32[1024,2048]{0,1:T(8,128)} %bitcast.38, f32[1,1,1024,1024]{3,2,1,0:T(8,128)} %param.7), kind=kOutput, calls=%fused_computation.3 | convolution fusion | flops 25769803776 | bytes 20971520 | tf_op jit(solution)/shard_map/dot_general | solution.py:20
  108.5 0.0 copy-done.4
  108.5 53.2 %fusion = bf16[2048,1024]{1,0:T(8,128)(2,1)S(1)} fusion(f32[1024,2048]{1,0:T(8,128)S(1)} %fusion.2, f32[1,1,1024,1024]{3,2,1,0:T(8,128)S(1)} %copy-done.4), kind=kOutput, calls=%fused_computation.1 | convolution fusion | flops 25769803776 | bytes 16777216 | tf_op jit(solution)/shard_map/dot_general | solution.py:23
  161.7 0.0 copy-done
  161.7 4.4 %fusion.6 = f32[2048,512]{1,0:T(8,128)} fusion(bf16[2048,1024]{1,0:T(8,128)(2,1)S(1)} %fusion, bf16[1,1,512,1024]{3,2,1,0:T(8,128)(2,1)S(1)} %copy-done), kind=kOutput, calls=%fused_computation.7 | convolution fusion | flops 2147483648 | bytes 9437184 | tf_op jit(solution)/shard_map/dot_general | solution.py:27
  166.1 5.2 %copy.22 = f32[512,4,512]{2,0,1:T(8,128)} copy(f32[512,4,512]{0,2,1:T(8,128)} %bitcast.39) | data formatting | bytes 8388608 | tf_op jit(solution)/shard_map/reshape | solution.py:52
  171.3 5.0 %gather_fusion = f32[4,512,512]{2,1,0:T(8,128)} fusion(f32[512,4,512]{2,0,1:T(8,128)} %copy.22, s32[1024]{0:T(1024)S(1)} %pad_clamp_fusion), kind=kCustom, calls=%fused_computation | custom fusion | bytes 8388624 | tf_op jit(solution)/shard_map/gather | solution.py:52
  176.3 6.8 %copy.23 = f32[512,4,512]{2,1,0:T(4,128)} copy(f32[512,4,512]{2,0,1:T(8,128)} %bitcast.37) | data formatting | bytes 8388608 | tf_op jit(solution)/shard_map/gather | solution.py:52
  183.1 0.0 copy-start.3
  183.1 6.1 %reshape_reshape.3 = f32[4,128,2048]{2,1,0:T(8,128)} reshape(f32[512,4,512]{2,1,0:T(4,128)} %copy.23) | data formatting | bytes 8388608 | tf_op jit(solution)/shard_map/reshape;reshape | solution.py:35
  189.2 0.0 copy-done.3
  189.2 9.9 %fusion.4 = f32[8,128,2048]{2,0,1:T(8,128)S(1)} fusion(f32[4,128,2048]{2,1,0:T(8,128)} %reshape_reshape.3, s32[4]{0:T(128)S(1)} %bitcast.40), kind=kOutput, calls=%fused_computation.5 | convolution fusion | flops 100663328 | bytes 12582928 | tf_op jit(solution)/shard_map/kb,kwp->bwp/dot_general | solution.py:36
  199.1 8.1 %copy.25 = f32[8,128,2048]{2,1,0:T(8,128)} copy(f32[8,128,2048]{2,0,1:T(8,128)S(1)} %fusion.4) | data formatting | bytes 16777216 | tf_op jit(solution)/shard_map/kb,kwp->bwp/dot_general | solution.py:36
  207.2 0.0 copy-start.1
  207.2 0.0 copy-start.2
  207.2 0.0 reduce-scatter.2.cloned.1.call-update
  207.2 147.6 %reduce-scatter.2.cloned.1.call-done = f32[128,2048]{1,0:T(8,128)} async-done(((f32[1024,2048]{1,0:T(8,128)}), f32[128,2048]{1,0:T(8,128)}) %reduce-scatter.2.cloned.1.call-update) | async-done | bytes 1048592 | tf_op jit(solution)/shard_map/reduce_scatter | solution.py:56
  354.8 0.0 copy-done.2
  354.8 2.3 fusion.9
  357.1 0.0 copy-done.1
  (2 shorter events, 0.0 us)
Async XLA Ops:
  6.5 155.2 %copy-start = (bf16[1,1,512,1024]{3,2,1,0:T(8,128)(2,1)S(1)}, bf16[1,1,512,1024]{3,2,1,0:T(8,128)(2,1)}, u32[]{:S(2)}) copy-start(bf16[1,1,512,1024]{3,2,1,0:T(8,128)(2,1)} %param.9) | copy-start | bytes 3145732
  6.5 63.4 %all-gather.3.cloned.1.call-start = ((), (), s32[]{:S(2)}) async-start(), calls=%async_computation.2 | async-start | bytes 10485760 | tf_op jit(solution)/shard_map/all_gather | solution.py:8
  7.3 347.5 %reduce-scatter.2.cloned.1.call-start = ((), (), s32[]{:S(2)}) async-start(), calls=%async_computation.1 | async-start | bytes 9437184 | tf_op jit(solution)/shard_map/reduce_scatter | solution.py:56
  78.6 29.8 %copy-start.4 = (f32[1,1,1024,1024]{3,2,1,0:T(8,128)S(1)}, f32[1,1,1024,1024]{3,2,1,0:T(8,128)}, u32[]{:S(2)}) copy-start(f32[1,1,1024,1024]{3,2,1,0:T(8,128)} %param.8) | copy-start | bytes 12582916
  183.1 6.1 %copy-start.3 = (s32[1,1,4]{2,1,0:T(1,128)S(1)}, s32[1,1,4]{2,1,0:T(1,128)}, u32[]{:S(2)}) copy-start(s32[1,1,4]{2,1,0:T(1,128)} %param.11) | copy-start | bytes 52
  207.2 149.9 %copy-start.1 = (bf16[1,1,512,1024]{3,2,1,0:T(8,128)(2,1)S(1)}, bf16[1,1,512,1024]{3,2,1,0:T(8,128)(2,1)}, u32[]{:S(2)}) copy-start(bf16[1,1,512,1024]{3,2,1,0:T(8,128)(2,1)} %param.9) | copy-start | bytes 3145732
  207.2 147.6 %copy-start.2 = (f32[1,128,2048]{2,1,0:T(8,128)S(1)}, f32[1,128,2048]{2,1,0:T(8,128)}, u32[]{:S(2)}) copy-start(f32[1,128,2048]{2,1,0:T(8,128)} %param.12) | copy-start | bytes 3145732
Sparse Core Ops, SparseCore 0:
  8.9 60.9 all-gather.2
  207.3 147.4 reduce-scatter.1
